TPU v7x, 8 devices: a whole 2x2x1 slice. The times are simulated.
8 devices in a mesh: dp: 1 (over z), w: 8 (over y, x, core).
Axes of the slice: x: 2, y: 2, z: 1, core: 2. Of those that a mesh axis runs over, the one named last changes fastest.
Arguments:
- hidden: bfloat16 [64, 256, 2048], P(('dp', 'w'))
- lengths: int32 [64], P(('dp', 'w'))
- attn_norm: bfloat16 [2, 2048], P(None, 'w')
- w_q: bfloat16 [2, 2048, 2048], P(None, 'w')
- w_k: bfloat16 [2, 2048, 256], P(None, 'w')
- w_v: bfloat16 [2, 2048, 256], P(None, 'w')
- w_o: bfloat16 [2, 2048, 2048], P(None, 'w')
- mlp_norm: bfloat16 [2, 2048], P(None, 'w')
- w_gate: bfloat16 [2, 2048, 16384], P(None, 'w')
- w_up: bfloat16 [2, 2048, 16384], P(None, 'w')
- w_down: bfloat16 [2, 16384, 2048], P(None, 'w')
Outputs:
- output 1: bfloat16 [64, 256, 2048], P(('dp', 'w'))
- output 2: bfloat16 [2, 64, 256, 1, 256], P(None, ('dp', 'w'))
- output 3: bfloat16 [2, 64, 256, 1, 256], P(None, ('dp', 'w'))
All inputs are finite; a program needn't handle non-finite values.
Results may differ from a plain program's by a relative error of at most 0.0138382.
Values are sent between devices in bfloat16 or wider.
A program may use at most 1 GiB of HBM per device.

v0:
```python
import jax
import jax.numpy as jnp
from jax import lax
from jax.sharding import PartitionSpec as P

HEAD_DIM = 256
RMS_EPS = 1e-6
ROPE_THETA = 10000.0
QUERY_BLOCK = 512


def rms_norm(hidden_f, norm_gain):
    mean_sq = jnp.mean(hidden_f * hidden_f, axis=-1, keepdims=True)
    return (hidden_f * lax.rsqrt(mean_sq + RMS_EPS) * (1.0 + norm_gain.astype(jnp.float32))).astype(jnp.bfloat16)


def rope_tables(seq_len):
    half_dim = HEAD_DIM // 2
    inv_freq = ROPE_THETA ** (-2.0 * jnp.arange(half_dim, dtype=jnp.float32) / HEAD_DIM)
    angles = jnp.arange(seq_len, dtype=jnp.float32)[:, None] * inv_freq[None, :]
    return jnp.cos(angles)[:, None, :], jnp.sin(angles)[:, None, :]


def apply_rope(projected, cos_tab, sin_tab):
    half_dim = HEAD_DIM // 2
    first_half = projected[..., :half_dim]
    second_half = projected[..., half_dim:]
    return jnp.concatenate([first_half * cos_tab - second_half * sin_tab, second_half * cos_tab + first_half * sin_tab], axis=-1)


def attention(q_rope, k_rope, v_proj, lengths):
    seq_len = q_rope.shape[1]
    q_block = min(seq_len, QUERY_BLOCK)
    pieces = []
    for q_start in range(0, seq_len, q_block):
        q_stop = q_start + q_block
        scores = jnp.einsum('bqhgd,bshd->bhgqs', q_rope[:, q_start:q_stop], k_rope[:, :q_stop], preferred_element_type=jnp.float32)
        q_pos = q_start + jnp.arange(q_block)
        k_pos = jnp.arange(q_stop)
        allowed = (k_pos[None, None, :] <= q_pos[None, :, None]) & (k_pos[None, None, :] < lengths[:, None, None])
        scores = jnp.where(allowed[:, None, None], scores, -1e30)
        scores = scores - jnp.max(scores, axis=-1, keepdims=True)
        exp_scores = jnp.exp(scores)
        attn_probs = exp_scores / jnp.sum(exp_scores, axis=-1, keepdims=True)
        row_live = q_pos[None, :] < lengths[:, None]
        attn_probs = jnp.where(row_live[:, None, None, :, None], attn_probs, 0.0).astype(jnp.bfloat16)
        pieces.append(jnp.einsum('bhgqs,bshd->bqhgd', attn_probs, v_proj[:, :q_stop], preferred_element_type=jnp.float32).astype(jnp.bfloat16))
    return jnp.concatenate(pieces, axis=1)


def mlp_block(mixed_bf, mlp_gain, wg_full, wu_full, wd_full):
    mixed_f = mixed_bf.astype(jnp.float32)
    normed = rms_norm(mixed_f, mlp_gain)
    gate_proj = jnp.einsum('bsd,df->bsf', normed, wg_full, preferred_element_type=jnp.float32)
    up_proj = jnp.einsum('bsd,df->bsf', normed, wu_full, preferred_element_type=jnp.float32)
    act_bf = (jax.nn.gelu(gate_proj, approximate=True) * up_proj).astype(jnp.bfloat16)
    return (mixed_f + jnp.einsum('bsf,fd->bsd', act_bf, wd_full, preferred_element_type=jnp.float32)).astype(jnp.bfloat16)


def layer_body(hidden, lengths, weights):
    attn_gain, wq_full, wk_full, wv_full, wo_full, mlp_gain, wg_full, wu_full, wd_full = weights
    n_seq = hidden.shape[0]
    seq_len = hidden.shape[1]
    n_heads = wq_full.shape[1] // HEAD_DIM
    kv_heads = wk_full.shape[1] // HEAD_DIM
    cos_tab, sin_tab = rope_tables(seq_len)
    hidden_f = hidden.astype(jnp.float32)
    normed = rms_norm(hidden_f, attn_gain)
    q_proj = jnp.einsum('bsd,de->bse', normed, wq_full, preferred_element_type=jnp.float32).reshape(n_seq, seq_len, n_heads, HEAD_DIM)
    k_proj = jnp.einsum('bsd,de->bse', normed, wk_full, preferred_element_type=jnp.float32).reshape(n_seq, seq_len, kv_heads, HEAD_DIM)
    v_proj = jnp.einsum('bsd,de->bse', normed, wv_full, preferred_element_type=jnp.float32).astype(jnp.bfloat16).reshape(n_seq, seq_len, kv_heads, HEAD_DIM)
    q_rope = (apply_rope(q_proj, cos_tab, sin_tab) * HEAD_DIM ** -0.5).astype(jnp.bfloat16).reshape(n_seq, seq_len, kv_heads, n_heads // kv_heads, HEAD_DIM)
    k_rope = apply_rope(k_proj, cos_tab, sin_tab).astype(jnp.bfloat16)
    attn_out = attention(q_rope, k_rope, v_proj, lengths).reshape(n_seq, seq_len, n_heads * HEAD_DIM)
    mixed_bf = (hidden_f + jnp.einsum('bse,ed->bsd', attn_out, wo_full, preferred_element_type=jnp.float32)).astype(jnp.bfloat16)
    return mlp_block(mixed_bf, mlp_gain, wg_full, wu_full, wd_full), k_rope, v_proj


def solution(mesh):
    batch_spec = P(('dp', 'w'))
    weight_spec = P(None, 'w')
    cache_spec = P(None, ('dp', 'w'))

    def device_fn(hidden, lengths, attn_norm, w_q, w_k, w_v, w_o, mlp_norm, w_gate, w_up, w_down):
        k_list = []
        v_list = []
        for layer_idx in range(w_q.shape[0]):
            gathered = [lax.all_gather(weight[layer_idx], 'w', axis=0, tiled=True) for weight in (attn_norm, w_q, w_k, w_v, w_o, mlp_norm, w_gate, w_up, w_down)]
            hidden, k_rope, v_proj = layer_body(hidden, lengths, gathered)
            k_list.append(k_rope)
            v_list.append(v_proj)
        return hidden, jnp.stack(k_list), jnp.stack(v_list)

    return jax.shard_map(device_fn, mesh=mesh, in_specs=(batch_spec, batch_spec) + (weight_spec,) * 9, out_specs=(batch_spec, cache_spec, cache_spec), check_vma=False)
```

profile of v0, /device:TPU:0, one launch (start us, length us, event | category | flops | bytes accessed | tf_op | source)
XLA Modules:
  0.0 2243.5 jit_solution(17186546907868178045)
XLA Ops:
  17.2 11.5 fusion.171
  28.8 11.5 fusion.170
  40.4 12.0 fusion.172
  57.3 13.7 all-gather
  76.9 10.9 all-gather.5
  88.4 10.8 all-gather.9
  99.9 11.3 all-gather.14
  124.7 24.8 %fusion.76 = f32[8,256,2048]{2,1,0:T(8,128)} fusion(bf16[1,2048,2048]{2,1,0:T(8,128)(2,1)} %all-gather.37.cloned.1.call-done, bf16[8,256,2048]{2,1,0:T(8,128)(2,1)} %param.11, f32[2048]{0:T(1024)S(1)} %bitcast.222, f32[8,256]{1,0:T(8,128)S(1)} %add_rsqrt_fusion.3), kind=kOutput, calls=%fused_computation.86 | convolution fusion | flops 17196646400 | bytes 33570816 | tf_op jit(solution)/shard_map/bsd,de->bse/dot_general | solution.py:69
  149.5 11.1 copy.72
  166.9 13.4 multiply_subtract_fusion.1
  180.2 11.2 fusion.58
  191.5 9.6 fusion.60
  201.1 10.2 fusion.102
  211.3 26.2 %fusion.44 = (f32[8,256]{1,0:T(8,128)S(1)}, bf16[8,256,2048]{2,1,0:T(8,128)(2,1)}) fusion(bf16[8,256,2048]{1,2,0:T(8,128)(2,1)} %bitcast.224, bf16[1,2048,2048]{2,1,0:T(8,128)(2,1)} %all-gather.39.cloned.1.call-done, bf16[8,256,2048]{2,1,0:T(8,128)(2,1)} %param.11), kind=kOutput, calls=%fused_computation.48 | convolution fusion | flops 17205032960 | bytes 33562624 | tf_op jit(solution)/shard_map/bse,ed->bsd/dot_general | solution.py:75
  237.5 212.5 %all-gather.43.cloned.1.call-done = bf16[1,2048,16384]{2,1,0:T(8,128)(2,1)} async-done(((bf16[1,256,16384]{2,1,0:T(8,128)(2,1)}), bf16[1,2048,16384]{2,1,0:T(8,128)(2,1)}) %all-gather.43.cloned.1.call-update) | async-done | bytes 67108880 | tf_op jit(solution)/shard_map/all_gather | solution.py:88
  450.0 151.2 %fusion.26 = f32[8,256,16384]{2,1,0:T(8,128)} fusion(bf16[1,2048,16384]{2,1,0:T(8,128)(2,1)} %all-gather.43.cloned.1.call-done, bf16[8,256,2048]{2,1,0:T(8,128)(2,1)} %get-tuple-element.44, f32[2048]{0:T(1024)S(1)} %bitcast.218, f32[8,256]{1,0:T(8,128)S(1)} %add_rsqrt_fusion.2), kind=kOutput, calls=%fused_computation.28 | convolution fusion | flops 137455730688 | bytes 209731584 | tf_op jit(solution)/shard_map/bsd,df->bsf/dot_general | solution.py:55
  601.2 147.7 %all-gather.41.cloned.1.call-done = bf16[1,2048,16384]{2,1,0:T(8,128)(2,1)} async-done(((bf16[1,256,16384]{2,1,0:T(8,128)(2,1)}), bf16[1,2048,16384]{2,1,0:T(8,128)(2,1)}) %all-gather.41.cloned.1.call-update) | async-done | bytes 67108880 | tf_op jit(solution)/shard_map/all_gather | solution.py:88
  748.9 188.6 %fusion.95.clone.4 = bf16[8,256,16384]{2,1,0:T(8,128)(2,1)} fusion(f32[8,256,16384]{2,1,0:T(8,128)} %fusion.26, bf16[1,2048,16384]{2,1,0:T(8,128)(2,1)} %all-gather.41.cloned.1.call-done, bf16[8,256,2048]{2,1,0:T(8,128)(2,1)} %get-tuple-element.44, f32[2048]{0:T(1024)S(1)} %bitcast.219, f32[8,256]{1,0:T(8,128)S(1)} %add_rsqrt_fusion.2), kind=kOutput, calls=%fused_computation.10.clone.clone.clone.clone.clone.clone.1 | convolution fusion | flops 137791275008 | bytes 276840448 | tf_op jit(solution)/shard_map/bsd,df->bsf/dot_general | solution.py:54
  937.5 110.4 %all-gather.45.cloned.1.call-done = bf16[1,16384,2048]{2,1,0:T(8,128)(2,1)} async-done(((bf16[1,2048,2048]{2,1,0:T(8,128)(2,1)}), bf16[1,16384,2048]{2,1,0:T(8,128)(2,1)}) %all-gather.45.cloned.1.call-update) | async-done | bytes 67108880 | tf_op jit(solution)/shard_map/all_gather | solution.py:88
  1047.9 152.8 %fusion.48 = (f32[8,256]{1,0:T(8,128)S(1)}, bf16[8,256,2048]{2,1,0:T(8,128)(2,1)}) fusion(bf16[1,16384,2048]{2,1,0:T(8,128)(2,1)} %all-gather.45.cloned.1.call-done, bf16[8,256,2048]{2,1,0:T(8,128)(2,1)} %get-tuple-element.44, bf16[8,256,16384]{2,1,0:T(8,128)(2,1)} %fusion.95.clone.4), kind=kOutput, calls=%fused_computation.52 | convolution fusion | flops 137464119296 | bytes 151003136 | tf_op jit(solution)/shard_map/bsf,fd->bsd/dot_general | solution.py:57
  1209.1 25.4 %fusion.70 = f32[8,256,2048]{1,2,0:T(8,128)} fusion(bf16[1,2048,2048]{2,1,0:T(8,128)(2,1)} %all-gather.51.cloned.1.call-done, bf16[8,256,2048]{2,1,0:T(8,128)(2,1)} %get-tuple-element.46, f32[2048]{0:T(1024)S(1)} %bitcast.216, f32[8,256]{1,0:T(8,128)S(1)} %add_rsqrt_fusion.1), kind=kOutput, calls=%fused_computation.80 | convolution fusion | flops 17196646400 | bytes 33570816 | tf_op jit(solution)/shard_map/bsd,de->bse/dot_general | solution.py:69
  1234.5 11.0 fusion.173
  1280.9 11.6 fusion.59
  1292.5 9.7 fusion.61
  1302.2 10.1 fusion.105
  1312.4 26.4 %fusion.52 = (f32[8,256]{1,0:T(8,128)S(1)}, bf16[8,256,2048]{2,1,0:T(8,128)(2,1)}) fusion(bf16[8,256,2048]{1,2,0:T(8,128)(2,1)} %bitcast.223, bf16[1,2048,2048]{2,1,0:T(8,128)(2,1)} %all-gather.53.cloned.1.call-done, bf16[8,256,2048]{2,1,0:T(8,128)(2,1)} %get-tuple-element.46), kind=kOutput, calls=%fused_computation.56 | convolution fusion | flops 17205032960 | bytes 33562624 | tf_op jit(solution)/shard_map/bse,ed->bsd/dot_general | solution.py:75
  1338.7 147.8 %all-gather.57.cloned.1.call-done = bf16[1,2048,16384]{2,1,0:T(8,128)(2,1)} async-done(((bf16[1,256,16384]{2,1,0:T(8,128)(2,1)}), bf16[1,2048,16384]{2,1,0:T(8,128)(2,1)}) %all-gather.57.cloned.1.call-update) | async-done | bytes 67108880 | tf_op jit(solution)/shard_map/all_gather | solution.py:88
  1486.5 151.3 %fusion.20 = f32[8,256,16384]{2,1,0:T(8,128)} fusion(bf16[1,2048,16384]{2,1,0:T(8,128)(2,1)} %all-gather.57.cloned.1.call-done, bf16[8,256,2048]{2,1,0:T(8,128)(2,1)} %get-tuple-element.50, f32[2048]{0:T(1024)S(1)} %bitcast.213, f32[8,256]{1,0:T(8,128)S(1)} %add_rsqrt_fusion), kind=kOutput, calls=%fused_computation.22 | convolution fusion | flops 137455730688 | bytes 209731584 | tf_op jit(solution)/shard_map/bsd,df->bsf/dot_general | solution.py:55
  1637.8 147.8 %all-gather.55.cloned.1.call-done = bf16[1,2048,16384]{2,1,0:T(8,128)(2,1)} async-done(((bf16[1,256,16384]{2,1,0:T(8,128)(2,1)}), bf16[1,2048,16384]{2,1,0:T(8,128)(2,1)}) %all-gather.55.cloned.1.call-update) | async-done | bytes 67108880 | tf_op jit(solution)/shard_map/all_gather | solution.py:88
  1785.6 188.4 %fusion.206 = bf16[8,256,16384]{2,1,0:T(8,128)(2,1)} fusion(f32[8,256,16384]{2,1,0:T(8,128)} %fusion.20, bf16[1,2048,16384]{2,1,0:T(8,128)(2,1)} %all-gather.55.cloned.1.call-done, bf16[8,256,2048]{2,1,0:T(8,128)(2,1)} %get-tuple-element.50, f32[2048]{0:T(1024)S(1)} %bitcast.214, f32[8,256]{1,0:T(8,128)S(1)} %add_rsqrt_fusion), kind=kOutput, calls=%fused_computation.19.clone.clone.clone.clone.1 | convolution fusion | flops 137791275008 | bytes 276840448 | tf_op jit(solution)/shard_map/bsd,df->bsf/dot_general | solution.py:54
  1974.0 111.1 %all-gather.59.cloned.1.call-done = bf16[1,16384,2048]{2,1,0:T(8,128)(2,1)} async-done(((bf16[1,2048,2048]{2,1,0:T(8,128)(2,1)}), bf16[1,16384,2048]{2,1,0:T(8,128)(2,1)}) %all-gather.59.cloned.1.call-update) | async-done | bytes 67108880 | tf_op jit(solution)/shard_map/all_gather | solution.py:88
  2085.0 151.6 %fusion.55 = bf16[8,256,2048]{2,1,0:T(8,128)(2,1)} fusion(bf16[8,256,2048]{2,1,0:T(8,128)(2,1)} %get-tuple-element.50, bf16[1,16384,2048]{2,1,0:T(8,128)(2,1)} %all-gather.59.cloned.1.call-done, bf16[8,256,16384]{2,1,0:T(8,128)(2,1)} %fusion.206), kind=kOutput, calls=%fused_computation.59 | convolution fusion | flops 137451536384 | bytes 150994944 | tf_op jit(solution)/shard_map/bsf,fd->bsd/dot_general | solution.py:57
  (129 shorter events, 85.4 us)
Async XLA Ops:
  7.2 105.0 %all-gather.35.cloned.1.call-start = ((), (), s32[]{:S(2)}) async-start(), calls=%async_computation.1 | async-start | bytes 1179648 | tf_op jit(solution)/shard_map/all_gather | solution.py:88
  9.0 109.1 %all-gather.33.cloned.1.call-start = ((), (), s32[]{:S(2)}) async-start(), calls=%async_computation | async-start | bytes 1179648 | tf_op jit(solution)/shard_map/all_gather | solution.py:88
  10.7 114.0 %all-gather.37.cloned.1.call-start = ((), (), s32[]{:S(2)}) async-start(), calls=%async_computation.2 | async-start | bytes 9437184 | tf_op jit(solution)/shard_map/all_gather | solution.py:88
  13.9 197.3 %all-gather.39.cloned.1.call-start = ((), (), s32[]{:S(2)}) async-start(), calls=%async_computation.3 | async-start | bytes 9437184 | tf_op jit(solution)/shard_map/all_gather | solution.py:88
  17.1 432.8 %all-gather.43.cloned.1.call-start = ((), (), s32[]{:S(2)}) async-start(), calls=%async_computation.5 | async-start | bytes 75497472 | tf_op jit(solution)/shard_map/all_gather | solution.py:88
  28.7 720.1 %all-gather.41.cloned.1.call-start = ((), (), s32[]{:S(2)}) async-start(), calls=%async_computation.4 | async-start | bytes 75497472 | tf_op jit(solution)/shard_map/all_gather | solution.py:88
  40.3 1007.6 %all-gather.45.cloned.1.call-start = ((), (), s32[]{:S(2)}) async-start(), calls=%async_computation.6 | async-start | bytes 75497472 | tf_op jit(solution)/shard_map/all_gather | solution.py:88
  52.4 1148.3 %all-gather.49.cloned.1.call-start = ((), (), s32[]{:S(2)}) async-start(), calls=%async_computation.8 | async-start | bytes 1179648 | tf_op jit(solution)/shard_map/all_gather | solution.py:88
  53.2 1155.9 %all-gather.51.cloned.1.call-start = ((), (), s32[]{:S(2)}) async-start(), calls=%async_computation.9 | async-start | bytes 9437184 | tf_op jit(solution)/shard_map/all_gather | solution.py:88
  54.0 1210.0 %all-gather.47.cloned.1.call-start = ((), (), s32[]{:S(2)}) async-start(), calls=%async_computation.7 | async-start | bytes 1179648 | tf_op jit(solution)/shard_map/all_gather | solution.py:88
  54.5 1257.8 %all-gather.53.cloned.1.call-start = ((), (), s32[]{:S(2)}) async-start(), calls=%async_computation.10 | async-start | bytes 9437184 | tf_op jit(solution)/shard_map/all_gather | solution.py:88
  55.3 1431.2 %all-gather.57.cloned.1.call-start = ((), (), s32[]{:S(2)}) async-start(), calls=%async_computation.12 | async-start | bytes 75497472 | tf_op jit(solution)/shard_map/all_gather | solution.py:88
  55.3 21.5 copy-start.27
  55.3 21.6 copy-start.26
  55.9 1729.7 %all-gather.55.cloned.1.call-start = ((), (), s32[]{:S(2)}) async-start(), calls=%async_computation.11 | async-start | bytes 75497472 | tf_op jit(solution)/shard_map/all_gather | solution.py:88
  56.6 2028.4 %all-gather.59.cloned.1.call-start = ((), (), s32[]{:S(2)}) async-start(), calls=%async_computation.13 | async-start | bytes 75497472 | tf_op jit(solution)/shard_map/all_gather | solution.py:88
  76.6 41.0 %copy-start.8 = (f32[256,128]{0,1:T(8,128)}, f32[256,128]{0,1:T(8,128)S(1)}, u32[]{:S(2)}) copy-start(f32[256,128]{0,1:T(8,128)S(1)} %get-tuple-element.39) | copy-start | bytes 393220
  76.6 41.0 %copy-start.10 = (f32[256,128]{0,1:T(8,128)}, f32[256,128]{0,1:T(8,128)S(1)}, u32[]{:S(2)}) copy-start(f32[256,128]{0,1:T(8,128)S(1)} %get-tuple-element.40) | copy-start | bytes 393220
  76.7 90.1 %copy-start.12 = (f32[256,128]{1,0:T(8,128)}, f32[256,128]{1,0:T(8,128)S(1)}, u32[]{:S(2)}) copy-start(f32[256,128]{1,0:T(8,128)S(1)} %copy.32) | copy-start | bytes 393220
  76.9 90.0 %copy-start.14 = (f32[256,128]{1,0:T(8,128)}, f32[256,128]{1,0:T(8,128)S(1)}, u32[]{:S(2)}) copy-start(f32[256,128]{1,0:T(8,128)S(1)} %copy.34) | copy-start | bytes 393220
  76.9 124.1 %copy-start.20 = (pred[8,256]{1,0:T(8,128)(4,1)}, pred[8,256]{1,0:T(8,128)(4,1)S(1)}, u32[]{:S(2)}) copy-start(pred[8,256]{1,0:T(8,128)(4,1)S(1)} %iota_compare_fusion.1) | copy-start | bytes 6148
  112.2 88.9 %copy-start.2 = (pred[8,256,256]{1,2,0:T(8,128)(4,1)}, pred[8,256,256]{1,2,0:T(8,128)(4,1)S(1)}, u32[]{:S(2)}) copy-start(pred[8,256,256]{1,2,0:T(8,128)(4,1)S(1)} %broadcast_and_fusion) | copy-start | bytes 1572868
  118.0 62.2 %copy-start.4 = (bf16[8,256,1,128]{1,3,0,2:T(8,128)(2,1)}, bf16[8,256,1,128]{1,3,0,2:T(8,128)(2,1)S(1)}, u32[]{:S(2)}) copy-start(bf16[8,256,1,128]{1,3,0,2:T(8,128)(2,1)S(1)} %get-tuple-element.25) | copy-start | bytes 1572868
  118.0 62.2 %copy-start.6 = (bf16[8,256,1,128]{1,3,0,2:T(8,128)(2,1)}, bf16[8,256,1,128]{1,3,0,2:T(8,128)(2,1)S(1)}, u32[]{:S(2)}) copy-start(bf16[8,256,1,128]{1,3,0,2:T(8,128)(2,1)S(1)} %get-tuple-element.26) | copy-start | bytes 1572868
  124.7 76.4 %copy-start.16 = (bf16[8,256,256]{2,1,0:T(8,128)(2,1)}, bf16[8,256,256]{2,1,0:T(8,128)(2,1)S(1)}, u32[]{:S(2)}) copy-start(bf16[8,256,256]{2,1,0:T(8,128)(2,1)S(1)} %fusion.134) | copy-start | bytes 3145732
  211.3 238.7 %copy-start.24 = (f32[1,2048]{1,0:T(1,128)S(1)}, f32[1,2048]{1,0:T(1,128)}, u32[]{:S(2)}) copy-start(f32[1,2048]{1,0:T(1,128)} %convert_add_fusion.6) | copy-start | bytes 24580
  1047.9 152.8 %copy-start.23 = (f32[1,2048]{1,0:T(1,128)S(1)}, f32[1,2048]{1,0:T(1,128)}, u32[]{:S(2)}) copy-start(f32[1,2048]{1,0:T(1,128)} %convert_add_fusion.5) | copy-start | bytes 24580
  1263.9 10.0 copy-start.1
  1270.4 10.5 copy-start.18
  1292.5 9.7 copy-start.19
  1292.5 9.7 copy-start.21
  1312.4 174.2 %copy-start.22 = (f32[1,2048]{1,0:T(1,128)S(1)}, f32[1,2048]{1,0:T(1,128)}, u32[]{:S(2)}) copy-start(f32[1,2048]{1,0:T(1,128)} %convert_add_fusion.4) | copy-start | bytes 24580
  (10 other events, 64.7 us)
Sparse Core Ops, SparseCore 0:
  9.8 20.4 all-gather.34
  32.1 17.5 all-gather.32
  52.1 48.8 all-gather.36
  102.6 48.3 all-gather.38
  152.7 297.1 all-gather.42
  451.6 297.1 all-gather.40
  750.7 297.1 all-gather.44
  1049.7 17.6 all-gather.48
  1069.8 48.3 all-gather.50
  1119.8 17.5 all-gather.46
  1139.3 48.3 all-gather.52
  1189.3 297.1 all-gather.56
  1488.3 297.1 all-gather.54
  1787.8 297.1 all-gather.58
where the time goes:
time: 2250 us; the launch traced here: 2240 us
  matrix products  1150 us (51%)
  waiting for transfers between devices  881 us (39%)
  local copies, waits for them, and re-layouts  96.9 us (4%)
  other arithmetic  50 us (2%)
  blocking collectives  46.7 us (2%)
    all_gather x14, waiting for transfers between devices, device_fn(): lax.all_gather(weight[layer_idx], 'w', axis=0, tiled=True)  877 us
    dot_general x2, matrix products, mlp_block(): jnp.einsum('bsd,df->bsf', normed, wg_full, preferred_element_type=jnp.flo...  377 us
    dot_general x2, matrix products, mlp_block(): jnp.einsum('bsf,fd->bsd', act_bf, wd_full, preferred_element_type=jnp.flo...  304 us
    dot_general x2, matrix products, mlp_block(): jnp.einsum('bsd,df->bsf', normed, wu_full, preferred_element_type=jnp.flo...  303 us
    dot_general x2, matrix products, layer_body(): jnp.einsum('bse,ed->bsd', attn_out, wo_full, preferred_element_type=jnp.f...  52.6 us
    dot_general x2, matrix products, layer_body(): jnp.einsum('bsd,de->bse', normed, wq_full, preferred_element_type=jnp.flo...  50.2 us
    all_gather x4, blocking collectives, device_fn(): lax.all_gather(weight[layer_idx], 'w', axis=0, tiled=True)  46.7 us
  transfers between devices with their start and end apart: 14, of which 6 were waited for; matrix products, arithmetic and copies ran while one was open for 51% of the time, Pallas kernels for 0%

commit v1 on v0

v1 whole, which is shorter than its diff:
```python
import functools

import jax
import jax.numpy as jnp
from jax import lax
from jax.experimental import pallas as pl
from jax.experimental.pallas import tpu as pltpu
from jax.sharding import PartitionSpec as P

HEAD_DIM = 256
RMS_EPS = 1e-6
ROPE_THETA = 10000.0
N_DEV = 8
CHUNKS = 16
CORE, XAX, YAX = 1, 2, 4
TILE = 512
PRE = (1, 3)
EXTRA = (1, 0)
MESH = pl.DeviceIdType.MESH
TO_X, TO_Y, TO_C, FWD_X, FWD_Y, C_X, C_Y, C_D = range(8)
KINDS = 8


def rms_norm(hidden_f, norm_gain):
    mean_sq = jnp.mean(hidden_f * hidden_f, axis=-1, keepdims=True)
    return (hidden_f * lax.rsqrt(mean_sq + RMS_EPS) * (1.0 + norm_gain.astype(jnp.float32))).astype(jnp.bfloat16)


def rope_tables(seq_len):
    half_dim = HEAD_DIM // 2
    inv_freq = ROPE_THETA ** (-2.0 * jnp.arange(half_dim, dtype=jnp.float32) / HEAD_DIM)
    angles = jnp.arange(seq_len, dtype=jnp.float32)[:, None] * inv_freq[None, :]
    return jnp.cos(angles)[:, None, :], jnp.sin(angles)[:, None, :]


def apply_rope(projected, cos_tab, sin_tab):
    half_dim = HEAD_DIM // 2
    first_half = projected[..., :half_dim]
    second_half = projected[..., half_dim:]
    return jnp.concatenate([first_half * cos_tab - second_half * sin_tab, second_half * cos_tab + first_half * sin_tab], axis=-1)


def attention(q_rope, k_rope, v_proj, lengths):
    seq_len = q_rope.shape[1]
    scores = jnp.einsum('bqhgd,bshd->bhgqs', q_rope, k_rope, preferred_element_type=jnp.float32)
    pos = jnp.arange(seq_len)
    allowed = (pos[None, None, :] <= pos[None, :, None]) & (pos[None, None, :] < lengths[:, None, None])
    scores = jnp.where(allowed[:, None, None], scores, -1e30)
    scores = scores - jnp.max(scores, axis=-1, keepdims=True)
    exp_scores = jnp.exp(scores)
    attn_probs = exp_scores / jnp.sum(exp_scores, axis=-1, keepdims=True)
    row_live = pos[None, :] < lengths[:, None]
    attn_probs = jnp.where(row_live[:, None, None, :, None], attn_probs, 0.0).astype(jnp.bfloat16)
    return jnp.einsum('bhgqs,bshd->bqhgd', attn_probs, v_proj, preferred_element_type=jnp.float32).astype(jnp.bfloat16)


def attn_block(hidden, lengths, gain, w_qkv, w_o):
    n_seq, seq_len, d_model = hidden.shape
    q_width = w_o.shape[0]
    n_heads = q_width // HEAD_DIM
    cos_tab, sin_tab = rope_tables(seq_len)
    hidden_f = hidden.astype(jnp.float32)
    normed = rms_norm(hidden_f, gain)
    proj = jnp.einsum('bsd,de->bse', normed, w_qkv, preferred_element_type=jnp.float32)
    q_proj = proj[..., :q_width].reshape(n_seq, seq_len, n_heads, HEAD_DIM)
    k_proj = proj[..., q_width:q_width + HEAD_DIM].reshape(n_seq, seq_len, 1, HEAD_DIM)
    v_proj = proj[..., q_width + HEAD_DIM:].astype(jnp.bfloat16).reshape(n_seq, seq_len, 1, HEAD_DIM)
    q_rope = (apply_rope(q_proj, cos_tab, sin_tab) * HEAD_DIM ** -0.5).astype(jnp.bfloat16).reshape(n_seq, seq_len, 1, n_heads, HEAD_DIM)
    k_rope = apply_rope(k_proj, cos_tab, sin_tab).astype(jnp.bfloat16)
    attn_out = attention(q_rope, k_rope, v_proj, lengths).reshape(n_seq, seq_len, q_width)
    mixed = (hidden_f + jnp.einsum('bse,ed->bsd', attn_out, w_o, preferred_element_type=jnp.float32)).astype(jnp.bfloat16)
    return mixed, k_rope, v_proj


def mlp_kernel(layer, n_ext, n_pre, n_own, n_extra, ext_at, wg_ref, wu_ref, wd_ref, pre_ref, ext_ref, m_ref, gain_ref, out_ref, gat_ref,
               acc, r2, wbuf, stage, ssem, rsem, ldsem, iosem):
    me = lax.axis_index('w')
    depth = wg_ref.shape[1]
    width = r2.shape[1]
    n_tok = r2.shape[0]
    rows, cols = wbuf.shape[1:]
    half = rows // 2
    wide = cols // N_DEV
    n_ready = n_ext + n_pre
    n_comm = n_own + n_extra
    n_steps = n_ready + n_own

    barrier = pltpu.get_barrier_semaphore()
    for axis in (CORE, XAX, YAX):
        pl.semaphore_signal(barrier, inc=1, device_id={'w': me ^ axis}, device_id_type=MESH)
    pl.semaphore_wait(barrier, 3)

    def remote(src, dst, kind, k, axis):
        return pltpu.make_async_remote_copy(src_ref=src, dst_ref=dst, send_sem=ssem.at[kind, k], recv_sem=rsem.at[kind, k],
                                            device_id={'w': me ^ axis}, device_id_type=MESH)

    def rcopy(kind, k):
        if kind in (TO_X, TO_Y, TO_C):
            src, axis = gat_ref.at[k, me], {TO_X: XAX, TO_Y: YAX, TO_C: CORE}[kind]
        elif kind == FWD_X:
            src, axis = gat_ref.at[k, me ^ YAX, pl.ds(0, half)], XAX
        elif kind == FWD_Y:
            src, axis = gat_ref.at[k, me ^ XAX, pl.ds(half, half)], YAX
        else:
            src, axis = gat_ref.at[k, me ^ {C_X: XAX, C_Y: YAX, C_D: XAX | YAX}[kind]], CORE
        return remote(src, src, kind, k, axis)

    def own_parts(lay, chunk, dst, put):
        def column_block(j, carry):
            at = pl.ds(pl.multiple_of(j * (wide * CHUNKS) + chunk * wide, wide), wide)
            to = pl.ds(pl.multiple_of(j * wide, wide), wide)
            put(wg_ref.at[lay, :, at], dst.at[pl.ds(0, depth), to])
            put(wu_ref.at[lay, :, at], dst.at[pl.ds(depth, depth), to])
            return carry

        lax.fori_loop(0, N_DEV, column_block, 0)
        down = pl.ds(pl.multiple_of(chunk * wide, wide), wide)
        for side in range(2):
            put(wd_ref.at[lay, down, pl.ds(side * cols, cols)], dst.at[pl.ds(2 * depth + side * wide, wide)])

    def chunk_of(k):
        if isinstance(k, int):
            return (layer, n_ready + k) if k < n_own else (layer + 1, k - n_own)
        if n_extra == 0:
            return layer, n_ready + k
        return jnp.where(k < n_own, layer, layer + 1), jnp.where(k < n_own, n_ready + k, k - n_own)

    def stage_a(k):
        lay, chunk = chunk_of(k)
        for kind, axis in ((TO_X, XAX), (TO_Y, YAX), (TO_C, CORE)):
            own_parts(lay, chunk, gat_ref.at[k, me], lambda src, dst: remote(src, dst, kind, k, axis).start())

    def stage_b(k):
        rcopy(TO_X, k).wait_recv()
        rcopy(FWD_Y, k).start()
        rcopy(C_X, k).start()
        rcopy(TO_Y, k).wait_recv()
        rcopy(FWD_X, k).start()
        rcopy(C_Y, k).start()

    def stage_c(k):
        rcopy(FWD_X, k).wait_recv()
        rcopy(FWD_Y, k).wait_recv()
        rcopy(C_D, k).start()
        for kind in (TO_C, C_X, C_Y, C_D):
            rcopy(kind, k).wait_recv()

    def load_gathered(ref, at, chunk):
        own_parts(layer, chunk, wbuf.at[me], lambda src, dst: pltpu.make_async_copy(src, dst, ldsem).start())
        for delta in range(1, N_DEV):
            pltpu.make_async_copy(ref.at[at, me ^ delta], wbuf.at[me ^ delta], ldsem).start()

    def event_at(s):
        if n_ready == 1:
            return s
        event = s + 1 - n_ready
        early = {1: 0, 2: 1, 4: 2, 5: 3}
        for at in range(n_ready + 3):
            event = jnp.where(s == at, early.get(at, -1), event)
        return event

    stage_a(0)
    stage_a(1)

    gain = 1.0 + gain_ref[...]

    def norm_tile(i, carry):
        tok = pl.ds(pl.multiple_of(i * TILE, TILE), TILE)
        copy = pltpu.make_async_copy(m_ref.at[tok], stage, iosem)
        copy.start()
        copy.wait()
        m_f = stage[...].astype(jnp.float32)
        acc[tok, :] = m_f
        mean_sq = jnp.mean(m_f * m_f, axis=-1, keepdims=True)
        r2[tok, :] = (m_f * lax.rsqrt(mean_sq + RMS_EPS) * gain).astype(jnp.bfloat16)
        return carry

    lax.fori_loop(0, n_tok // TILE, norm_tile, 0)

    def step(s, carry):
        k = s - n_ready
        last = s == n_steps - 1

        event = event_at(s)

        @pl.when((event >= 0) & (event < n_comm))
        def _():
            stage_b(event)

        @pl.when((event >= 0) & (event + 2 < n_comm))
        def _():
            stage_a(event + 2)

        @pl.when(event >= 1)
        def _():
            stage_c(event - 1)

        @pl.when(k >= 0)
        def _():
            load_gathered(gat_ref, k, s)

        if n_ext:
            @pl.when(s < n_ext)
            def _():
                load_gathered(ext_ref, ext_at + s, s)

        if n_pre:
            @pl.when((s >= n_ext) & (s < n_ready))
            def _():
                for dev in range(N_DEV):
                    pltpu.make_async_copy(pre_ref.at[dev, s - n_ext], wbuf.at[dev], ldsem).start()

        pltpu.make_async_copy(gat_ref.at[0], wbuf, ldsem).wait()

        def tile_step(i, inner):
            tok = pl.ds(pl.multiple_of(i * TILE, TILE), TILE)
            r_t = r2[tok, :]
            gate = jnp.dot(r_t, wbuf[:, 0:depth, :].reshape(width, cols), preferred_element_type=jnp.float32)
            up = jnp.dot(r_t, wbuf[:, depth:2 * depth, :].reshape(width, cols), preferred_element_type=jnp.float32)
            act = (jax.nn.gelu(gate, approximate=True) * up).astype(jnp.bfloat16)
            for side in range(2):
                lo = 2 * depth + side * wide
                w_down = wbuf[:, lo:lo + wide, :].reshape(N_DEV * wide, cols)
                acc[tok, pl.ds(side * cols, cols)] += jnp.dot(act, w_down, preferred_element_type=jnp.float32)

            @pl.when(last)
            def _():
                @pl.when(i > 0)
                def _():
                    pltpu.make_async_copy(stage, out_ref.at[tok], iosem).wait()
                stage[...] = acc[tok, :].astype(jnp.bfloat16)
                pltpu.make_async_copy(stage, out_ref.at[tok], iosem).start()
            return inner

        lax.fori_loop(0, n_tok // TILE, tile_step, 0)
        return carry

    lax.fori_loop(0, n_steps, step, 0)
    pltpu.make_async_copy(stage, out_ref.at[pl.ds(0, TILE)], iosem).wait()

    for k in range(n_own, n_comm):
        if k > n_own:
            stage_b(k)
        stage_c(k)

    def drain(k, carry):
        for kind in range(KINDS):
            rcopy(kind, k).wait_send()
        return carry

    lax.fori_loop(0, n_comm, drain, 0)


def mlp_call(layer, w_gate, w_up, w_down, pre, ext, ext_at, mixed, gain):
    n_seq, seq_len, d_model = mixed.shape
    n_tok = n_seq * seq_len
    d_ff = w_gate.shape[2]
    depth = w_gate.shape[1]
    cols = d_ff // CHUNKS
    rows = 2 * depth + 2 * cols // N_DEV
    n_ext = EXTRA[layer - 1] if layer > 0 else 0
    n_extra = EXTRA[layer]
    n_pre = PRE[layer]
    n_own = CHUNKS - n_ext - n_pre
    out, gathered = pl.pallas_call(
        functools.partial(mlp_kernel, layer, n_ext, n_pre, n_own, n_extra, ext_at),
        out_shape=(jax.ShapeDtypeStruct((n_tok, d_model), jnp.bfloat16),
                   jax.ShapeDtypeStruct((n_own + n_extra, N_DEV, rows, cols), jnp.bfloat16)),
        in_specs=[pl.BlockSpec(memory_space=pl.ANY)] * 6 + [pl.BlockSpec(memory_space=pltpu.VMEM)],
        out_specs=[pl.BlockSpec(memory_space=pl.ANY)] * 2,
        scratch_shapes=[
            pltpu.VMEM((n_tok, d_model), jnp.float32),
            pltpu.VMEM((n_tok, d_model), jnp.bfloat16),
            pltpu.VMEM((N_DEV, rows, cols), jnp.bfloat16),
            pltpu.VMEM((TILE, d_model), jnp.bfloat16),
            pltpu.SemaphoreType.DMA((KINDS, n_own + n_extra)),
            pltpu.SemaphoreType.DMA((KINDS, n_own + n_extra)),
            pltpu.SemaphoreType.DMA,
            pltpu.SemaphoreType.DMA,
        ],
        compiler_params=pltpu.CompilerParams(collective_id=layer, has_side_effects=True, vmem_limit_bytes=63 * 1024 * 1024),
        cost_estimate=pl.CostEstimate(flops=6 * n_tok * d_model * d_ff, bytes_accessed=12 * d_model * d_ff, transcendentals=0),
        name=f'mlp_gather_{layer}',
    )(w_gate, w_up, w_down, pre, ext, mixed.reshape(n_tok, d_model), (gain.astype(jnp.float32)).reshape(1, d_model))
    return out.reshape(n_seq, seq_len, d_model), gathered, n_own


def pack_kernel(layer, first, wg_ref, wu_ref, wd_ref, out_ref, sem):
    depth = wg_ref.shape[1]
    count, _, cols = out_ref.shape
    wide = cols // N_DEV
    for i in range(count):
        chunk = first + i
        for j in range(N_DEV):
            at = pl.ds(j * wide * CHUNKS + chunk * wide, wide)
            to = pl.ds(j * wide, wide)
            pltpu.make_async_copy(wg_ref.at[layer, :, at], out_ref.at[i, pl.ds(0, depth), to], sem).start()
            pltpu.make_async_copy(wu_ref.at[layer, :, at], out_ref.at[i, pl.ds(depth, depth), to], sem).start()
        for side in range(2):
            src = wd_ref.at[layer, pl.ds(chunk * wide, wide), pl.ds(side * cols, cols)]
            pltpu.make_async_copy(src, out_ref.at[i, pl.ds(2 * depth + side * wide, wide)], sem).start()
    pltpu.make_async_copy(out_ref, out_ref, sem).wait()


def own_pieces(layer, first, count, w_gate, w_up, w_down):
    depth = w_gate.shape[1]
    cols = w_gate.shape[2] // CHUNKS
    rows = 2 * depth + 2 * cols // N_DEV
    return pl.pallas_call(
        functools.partial(pack_kernel, layer, first),
        out_shape=jax.ShapeDtypeStruct((count, rows, cols), jnp.bfloat16),
        in_specs=[pl.BlockSpec(memory_space=pl.ANY)] * 3,
        out_specs=pl.BlockSpec(memory_space=pltpu.VMEM),
        scratch_shapes=[pltpu.SemaphoreType.DMA],
        name=f'pack_{layer}',
    )(w_gate, w_up, w_down)


def solution(mesh):
    batch_spec = P(('dp', 'w'))
    weight_spec = P(None, 'w')
    cache_spec = P(None, ('dp', 'w'))

    def device_fn(hidden, lengths, attn_norm, w_q, w_k, w_v, w_o, mlp_norm, w_gate, w_up, w_down):
        n_layers = w_q.shape[0]
        gains = lax.all_gather(jnp.concatenate([attn_norm, mlp_norm], axis=0), 'w', axis=1, tiled=True)
        k_list = []
        v_list = []
        ext, ext_at = None, 0
        for layer in range(n_layers):
            qkv_own = jnp.concatenate([w_q[layer], w_k[layer], w_v[layer]], axis=1)
            w_qkv_full = lax.all_gather(qkv_own, 'w', axis=0, tiled=True)
            w_o_full = lax.all_gather(w_o[layer], 'w', axis=0, tiled=True)
            n_ext = EXTRA[layer - 1] if layer > 0 else 0
            pre_own = own_pieces(layer, n_ext, PRE[layer], w_gate, w_up, w_down)
            if layer > 0:
                pre_own, hidden = lax.optimization_barrier((pre_own, hidden))
            pre = lax.all_gather(pre_own, 'w', axis=0, tiled=False)
            mixed, k_rope, v_proj = attn_block(hidden, lengths, gains[layer], w_qkv_full, w_o_full)
            hidden, ext, ext_at = mlp_call(layer, w_gate, w_up, w_down, pre, pre if ext is None else ext, ext_at, mixed, gains[n_layers + layer])
            k_list.append(k_rope)
            v_list.append(v_proj)
        return hidden, jnp.stack(k_list), jnp.stack(v_list)

    return jax.shard_map(device_fn, mesh=mesh, in_specs=(batch_spec, batch_spec) + (weight_spec,) * 9, out_specs=(batch_spec, cache_spec, cache_spec), check_vma=False)
```

time: 2250 us -> 1970 us (0.88)
  Pallas kernels: 0 us -> 1590 us
  matrix products: 1150 us -> 145 us
  waiting for transfers between devices: 881 us -> 41.6 us
  blocking collectives: 46.7 us -> 13.8 us
    pallas_call x0 -> x4, Pallas kernels: none -> 1590 us  [the longest x2 1580 us: mlp_call(): pl.pallas_call(functools.partial(mlp_kernel, layer, n_ext, n_pre, n_own,...]
    dot_general x18 -> x8, matrix products: 1150 us -> 145 us  [the longest x2 52.8 us: attn_block(): jnp.einsum('bsd,de->bse', normed, w_qkv, preferred_element_type=jnp.float32)]
    all_gather x14 -> x6, waiting for transfers between devices: 877 us -> 41 us  [the longest x2 27.1 us: device_fn(): w_qkv_full = lax.all_gather(qkv_own, 'w', axis=0, tiled=True)]
    all_gather x4 -> x1, blocking collectives: 46.7 us -> 13.8 us  [device_fn(): lax.all_gather(jnp.concatenate([attn_norm, mlp_norm], axis=0), 'w', axis=...]
    unnamed x62 -> x46, local copies, waits for them, and re-layouts: 35.4 us -> 46.3 us
  transfers between devices with their start and end apart: 14 -> 6, of which waited for: 6 -> 3; matrix products, arithmetic and copies ran while one was open for 51% -> 14% of each run, Pallas kernels for 0% -> 47%
where the time goes in v1:
time: 1970 us; the launch traced here: 1960 us
  Pallas kernels  1590 us (81%)
  matrix products  145 us (7%)
  local copies, waits for them, and re-layouts  98.9 us (5%)
  other arithmetic  59.5 us (3%)
  waiting for transfers between devices  41.6 us (2%)
    pallas_call x2, Pallas kernels, mlp_call(): pl.pallas_call(functools.partial(mlp_kernel, layer, n_ext, n_pre, n_own,...  1580 us
    dot_general x2, matrix products, attn_block(): jnp.einsum('bsd,de->bse', normed, w_qkv, preferred_element_type=jnp.float32)  52.8 us
    dot_general x2, matrix products, attn_block(): jnp.einsum('bse,ed->bsd', attn_out, w_o, preferred_element_type=jnp.float32)  49 us
    unnamed x46, local copies, waits for them, and re-layouts  46.3 us
  transfers between devices with their start and end apart: 6, of which 3 were waited for; matrix products, arithmetic and copies ran while one was open for 14% of the time, Pallas kernels for 47%

profile of v1, /device:TPU:0, one launch (start us, length us, event | category | flops | bytes accessed | tf_op | source)
XLA Modules:
  0.0 1962.6 jit_solution(5623343364223216370)
XLA Ops:
  13.0 2.6 pack_0.1
  17.6 13.8 all_gather.29
  32.6 4.6 pack_1.1
  37.3 5.1 fusion
  44.9 27.0 %all-gather.11.cloned.1.call-done = bf16[2048,2560]{1,0:T(8,128)(2,1)} async-done(((bf16[256,2560]{1,0:T(8,128)(2,1)}), bf16[2048,2560]{1,0:T(8,128)(2,1)}) %all-gather.11.cloned.1.call-update) | async-done | bytes 10485776 | tf_op jit(solution)/shard_map/all_gather | solution.py:332
  72.0 26.4 %fusion.16 = f32[8,256,2560]{2,1,0:T(8,128)S(1)} fusion(bf16[2048,2560]{1,0:T(8,128)(2,1)} %all-gather.11.cloned.1.call-done, bf16[8,256,2048]{2,1,0:T(8,128)(2,1)} %param.11, f32[2048]{0:T(1024)S(1)} %bitcast.161, f32[8,256]{1,0:T(8,128)S(1)} %add_rsqrt_fusion.1), kind=kOutput, calls=%fused_computation.30 | convolution fusion | flops 21491613696 | bytes 39862272 | tf_op jit(solution)/shard_map/bsd,de->bse/dot_general | solution.py:64
  100.3 5.1 copy-done.1
  105.4 6.0 copy.66
  111.4 6.5 fusion.81
  119.2 12.1 multiply_subtract_fusion.1
  131.3 10.1 fusion.10
  141.4 9.7 fusion.12
  151.1 11.0 fusion.48
  162.1 24.4 %fusion.3 = bf16[8,256,2048]{2,1,0:T(8,128)(2,1)} fusion(bf16[8,256,2048]{2,1,0:T(8,128)(2,1)} %param.11, bf16[8,256,2048]{1,2,0:T(8,128)(2,1)} %bitcast.168, bf16[1,2048,2048]{2,1,0:T(8,128)(2,1)} %all-gather.17.cloned.1.call-done), kind=kOutput, calls=%fused_computation.9 | convolution fusion | flops 17192452096 | bytes 33554432 | tf_op jit(solution)/shard_map/bse,ed->bsd/dot_general | solution.py:71
  186.5 4.4 all-gather.15.cloned.1.call-done
  190.8 914.5 %mlp_gather_0.1 = (bf16[2048,2048]{1,0:T(8,128)(2,1)}, bf16[16,8,768,1024]{3,2,1,0:T(8,128)(2,1)}) custom-call(bf16[2,256,16384]{2,1,0:T(8,128)(2,1)} %wg_ref.7, bf16[2,256,16384]{2,1,0:T(8,128)(2,1)} %wu_ref.7, bf16[2,2048,2048]{2,1,0:T(8,128)(2,1)} %wd_ref.7, bf16[8,1,768,1024]{3,2,1,0:T(8,128)(2,1)} %bitcast.163, bf16[8,1,768,1024]{3,2,1,0:T(8,128)(2,1)} %bitcast.164, ...), custom_call_target="tpu_custom_call" | custom-call | flops 412316860416 | bytes 402653184 | tf_op jit(solution)/shard_map/mlp_gather_0/pallas_call | solution.py:265
  1107.1 5.1 fusion.4
  1112.3 26.4 %fusion.14 = f32[8,256,2560]{2,1,0:T(8,128)S(1)} fusion(bf16[2048,2560]{1,0:T(8,128)(2,1)} %all-gather.13.cloned.1.call-done, bf16[8,256,2048]{2,1,0:T(8,128)(2,1)} %bitcast.149, f32[2048]{0:T(1024)S(1)} %bitcast.160, f32[8,256]{1,0:T(8,128)S(1)} %add_rsqrt_fusion), kind=kOutput, calls=%fused_computation.28 | convolution fusion | flops 21491613696 | bytes 39862272 | tf_op jit(solution)/shard_map/bsd,de->bse/dot_general | solution.py:64
  1138.7 7.0 copy-done.2
  1145.7 6.1 slice.120
  1151.8 16.4 copy.42
  1168.2 11.2 fusion.80
  1179.4 9.2 copy.65
  1188.5 9.1 copy.64
  1206.9 7.2 multiply_subtract_fusion
  1214.1 10.7 fusion.11
  1224.8 9.6 fusion.13
  1234.4 11.0 fusion.51
  1245.4 24.6 %fusion.7 = bf16[8,256,2048]{2,1,0:T(8,128)(2,1)} fusion(bf16[8,256,2048]{2,1,0:T(8,128)(2,1)} %bitcast.150, bf16[8,256,2048]{1,2,0:T(8,128)(2,1)} %bitcast.166, bf16[1,2048,2048]{2,1,0:T(8,128)(2,1)} %all-gather.21.cloned.1.call-done), kind=kOutput, calls=%fused_computation.13 | convolution fusion | flops 17192452096 | bytes 33554432 | tf_op jit(solution)/shard_map/bse,ed->bsd/dot_general | solution.py:71
  1270.0 9.5 all-gather.19.cloned.1.call-done
  1279.6 667.3 %mlp_gather_1.1 = (bf16[2048,2048]{1,0:T(8,128)(2,1)}, bf16[12,8,768,1024]{3,2,1,0:T(8,128)(2,1)}) custom-call(bf16[2,256,16384]{2,1,0:T(8,128)(2,1)} %wg_ref.7, bf16[2,256,16384]{2,1,0:T(8,128)(2,1)} %wu_ref.7, bf16[2,2048,2048]{2,1,0:T(8,128)(2,1)} %wd_ref.7, bf16[8,3,768,1024]{3,2,1,0:T(8,128)(2,1)} %bitcast.162, ...), custom_call_target="tpu_custom_call" | custom-call | flops 412316860416 | bytes 402653184 | tf_op jit(solution)/shard_map/mlp_gather_1/pallas_call | solution.py:265
  1946.9 8.4 copy.72
  (80 shorter events, 25.6 us)
Async XLA Ops:
  7.2 4.3 copy-start.9
  7.2 64.8 %all-gather.11.cloned.1.call-start = ((), (), s32[]{:S(2)}) async-start(), calls=%async_computation | async-start | bytes 11796480 | tf_op jit(solution)/shard_map/all_gather | solution.py:332
  11.4 150.7 %all-gather.17.cloned.1.call-start = ((), (), s32[]{:S(2)}) async-start(), calls=%async_computation.3 | async-start | bytes 9437184 | tf_op jit(solution)/shard_map/all_gather | solution.py:333
  12.9 4.6 copy-start.16
  12.9 4.6 copy-start.17
  12.9 177.9 %all-gather.15.cloned.1.call-start = ((), (), s32[]{:S(2)}) async-start(), calls=%async_computation.2 | async-start | bytes 14155776 | tf_op jit(solution)/shard_map/all_gather | solution.py:338
  15.7 1096.6 %all-gather.13.cloned.1.call-start = ((), (), s32[]{:S(2)}) async-start(), calls=%async_computation.1 | async-start | bytes 11796480 | tf_op jit(solution)/shard_map/all_gather | solution.py:332
  16.9 1228.5 %all-gather.21.cloned.1.call-start = ((), (), s32[]{:S(2)}) async-start(), calls=%async_computation.5 | async-start | bytes 9437184 | tf_op jit(solution)/shard_map/all_gather | solution.py:333
  17.5 1262.1 %all-gather.19.cloned.1.call-start = ((), (), s32[]{:S(2)}) async-start(), calls=%async_computation.4 | async-start | bytes 42467328 | tf_op jit(solution)/shard_map/all_gather | solution.py:338
  32.6 4.6 copy-start.18
  37.3 113.7 %copy-start.13 = (pred[8,256]{1,0:T(8,128)(4,1)}, pred[8,256]{1,0:T(8,128)(4,1)S(1)}, u32[]{:S(2)}) copy-start(pred[8,256]{1,0:T(8,128)(4,1)S(1)} %iota_compare_fusion.1) | copy-start | bytes 6148
  43.6 75.6 %copy-start.5 = (f32[256,128]{1,0:T(8,128)}, f32[256,128]{1,0:T(8,128)S(1)}, u32[]{:S(2)}) copy-start(f32[256,128]{1,0:T(8,128)S(1)} %get-tuple-element.46) | copy-start | bytes 393220
  98.4 7.0 copy-start.1
  111.4 6.5 copy-start.7
  119.2 12.1 copy-start.3
  119.2 12.1 copy-start.10
  1105.4 6.9 copy-start.15
  1138.7 7.0 copy-start.2
  1197.7 5.9 copy-start.6
  1197.7 5.9 copy-start.8
  1197.7 6.2 copy-start.11
  1197.7 6.2 copy-start.12
  1197.7 7.9 copy-start
  1199.5 6.0 slice-start
  1201.1 5.9 slice-start.1
  1206.9 7.2 copy-start.4
  1224.8 9.6 copy-start.14
Sparse Core Ops, SparseCore 0:
  11.5 60.4 all-gather.10
  73.8 48.3 all-gather.16
  124.5 66.2 all-gather.14
  192.5 100.2 all-gather.12
  294.4 82.7 all-gather.20
  1105.5 173.9 all-gather.18

commit v2 on v0

v2 whole, which is shorter than its diff:
```python
import functools

import jax
import jax.numpy as jnp
from jax import lax
from jax.experimental import pallas as pl
from jax.experimental.pallas import tpu as pltpu
from jax.sharding import PartitionSpec as P

HEAD_DIM = 256
RMS_EPS = 1e-6
ROPE_THETA = 10000.0
N_DEV = 8
CHUNKS = 16
CORE, XAX, YAX = 1, 2, 4
TILE = 512
PRE = 2
GAIN_ROWS = 8
MESH = pl.DeviceIdType.MESH
TO_X, TO_Y, TO_C, FWD_X, FWD_Y, C_X, C_Y, C_D = range(8)
KINDS = 8


def rope_tables(seq_len):
    half_dim = HEAD_DIM // 2
    inv_freq = ROPE_THETA ** (-2.0 * jnp.arange(half_dim, dtype=jnp.float32) / HEAD_DIM)
    angles = jnp.arange(seq_len, dtype=jnp.float32)[:, None] * inv_freq[None, :]
    return jnp.cos(angles), jnp.sin(angles)


class Gather:
    def __init__(self, gat_ref, ssem, rsem, half):
        self.me = lax.axis_index('w')
        self.gat, self.ssem, self.rsem, self.half = gat_ref, ssem, rsem, half

    def remote(self, src, dst, kind, k, axis):
        return pltpu.make_async_remote_copy(src_ref=src, dst_ref=dst, send_sem=self.ssem.at[kind, k], recv_sem=self.rsem.at[kind, k],
                                            device_id={'w': self.me ^ axis}, device_id_type=MESH)

    def rcopy(self, kind, k):
        me, half = self.me, self.half
        if kind in (TO_X, TO_Y, TO_C):
            src, axis = self.gat.at[k, me], {TO_X: XAX, TO_Y: YAX, TO_C: CORE}[kind]
        elif kind == FWD_X:
            src, axis = self.gat.at[k, me ^ YAX, pl.ds(0, half)], XAX
        elif kind == FWD_Y:
            src, axis = self.gat.at[k, me ^ XAX, pl.ds(half, self.gat.shape[2] - half)], YAX
        else:
            src, axis = self.gat.at[k, me ^ {C_X: XAX, C_Y: YAX, C_D: XAX | YAX}[kind]], CORE
        return self.remote(src, src, kind, k, axis)

    def stage_a(self, k, parts):
        for kind, axis in ((TO_X, XAX), (TO_Y, YAX), (TO_C, CORE)):
            parts(self.gat.at[k, self.me], lambda src, dst: self.remote(src, dst, kind, k, axis).start())

    def stage_b(self, k):
        self.rcopy(TO_X, k).wait_recv()
        self.rcopy(FWD_Y, k).start()
        self.rcopy(C_X, k).start()
        self.rcopy(TO_Y, k).wait_recv()
        self.rcopy(FWD_X, k).start()
        self.rcopy(C_Y, k).start()

    def stage_c(self, k):
        self.rcopy(FWD_X, k).wait_recv()
        self.rcopy(FWD_Y, k).wait_recv()
        self.rcopy(C_D, k).start()
        for kind in (TO_C, C_X, C_Y, C_D):
            self.rcopy(kind, k).wait_recv()

    def drain(self, count):
        def one(k, carry):
            for kind in range(KINDS):
                self.rcopy(kind, k).wait_send()
            return carry

        lax.fori_loop(0, count, one, 0)


def greet():
    barrier = pltpu.get_barrier_semaphore()
    for axis in (CORE, XAX, YAX):
        pl.semaphore_signal(barrier, inc=1, device_id={'w': lax.axis_index('w') ^ axis}, device_id_type=MESH)
    pl.semaphore_wait(barrier, 3)


def chunk_parts(layer, chunk, mlp_refs, dst, put):
    wg_ref, wu_ref, wd_ref = mlp_refs
    depth, cols = wg_ref.shape[1], wg_ref.shape[2] // CHUNKS
    wide = cols // N_DEV

    def column_block(j, carry):
        at = pl.ds(pl.multiple_of(j * (wide * CHUNKS) + chunk * wide, wide), wide)
        to = pl.ds(pl.multiple_of(j * wide, wide), wide)
        put(wg_ref.at[layer, :, at], dst.at[pl.ds(0, depth), to])
        put(wu_ref.at[layer, :, at], dst.at[pl.ds(depth, depth), to])
        return carry

    lax.fori_loop(0, N_DEV, column_block, 0)
    down = pl.ds(pl.multiple_of(chunk * wide, wide), wide)
    for side in range(2):
        put(wd_ref.at[layer, down, pl.ds(side * cols, cols)], dst.at[pl.ds(2 * depth + side * wide, wide)])


def attn_parts(layer, attn_refs, dst, put):
    at = 0
    depth = attn_refs[0].shape[1]
    for ref in attn_refs[:-1]:
        put(ref.at[layer], dst.at[pl.ds(0, depth), pl.ds(at, ref.shape[2])])
        at += ref.shape[2]
    put(attn_refs[-1], dst.at[pl.ds(depth, GAIN_ROWS)])


def attn_kernel(layer, n_layers, len_ref, wg_ref, wu_ref, wd_ref, wq_ref, wk_ref, wv_ref, wo_ref, ng_ref, full_ref, h_ref, cos_ref, sin_ref,
                m_ref, k_ref, v_ref, gain_ref, gat_ref, *rest):
    if layer == 0:
        attn_gat, w_v, h_v, m_v, o_v, ssem, rsem, wsem, hsem, msem, att_s, att_r = rest
    else:
        w_v, h_v, m_v, o_v, ssem, rsem, wsem, hsem, msem = rest
        attn_gat = full_ref
    me = lax.axis_index('w')
    count = gat_ref.shape[0]
    n_seq, seq_len, head_dim = k_ref.shape
    q_width = o_v.shape[1]
    d_model = h_v.shape[1]
    depth = wq_ref.shape[1]
    half = head_dim // 2
    mlp_refs = wg_ref, wu_ref, wd_ref
    attn_refs = wq_ref, wk_ref, wv_ref, wo_ref, ng_ref
    comm = Gather(gat_ref, ssem, rsem, gat_ref.shape[2] // 2)
    greet()
    load_h = pltpu.make_async_copy(h_ref, h_v, hsem)
    load_h.start()
    if layer == 0:
        first = Gather(attn_gat, att_s, att_r, depth // 2)
        first.stage_a(0, functools.partial(attn_parts, layer, attn_refs))
        first.stage_b(0)
    for k in range(count):
        comm.stage_a(k, functools.partial(chunk_parts, layer, k, mlp_refs))
    if layer == 0:
        first.stage_c(0)
    attn_parts(layer, attn_refs, w_v.at[me], lambda src, dst: pltpu.make_async_copy(src, dst, wsem).start())
    for delta in range(1, N_DEV):
        pltpu.make_async_copy(attn_gat.at[0, me ^ delta], w_v.at[me ^ delta], wsem).start()
    load_h.wait()
    pltpu.make_async_copy(attn_gat.at[0], w_v, wsem).wait()

    def gain_of(at):
        rows = [w_v[dev, depth:depth + GAIN_ROWS, 0:depth].astype(jnp.float32)[at:at + 1] for dev in range(N_DEV)]
        return jnp.concatenate(rows, axis=1)

    gain = 1.0 + gain_of(layer)
    gain_ref[...] = gain_of(n_layers + layer)
    row = lax.broadcasted_iota(jnp.int32, (seq_len, seq_len), 0)
    col = lax.broadcasted_iota(jnp.int32, (seq_len, seq_len), 1)

    def prompt(p, carry):
        @pl.when(p == 3)
        def _():
            comm.stage_b(0)

        @pl.when(p == 6)
        def _():
            comm.stage_b(1)
            comm.stage_c(0)

        tok = pl.ds(pl.multiple_of(p * seq_len, seq_len), seq_len)
        h_f = h_v[tok, :].astype(jnp.float32)
        mean_sq = jnp.mean(h_f * h_f, axis=-1, keepdims=True)
        normed = (h_f * lax.rsqrt(mean_sq + RMS_EPS) * gain).astype(jnp.bfloat16)
        cos, sin = cos_ref[...], sin_ref[...]

        def rope(x):
            a, c = x[:, :half], x[:, half:]
            return jnp.concatenate([a * cos - c * sin, c * cos + a * sin], axis=-1)

        kv = jnp.dot(normed, w_v[:, 0:depth, q_width:q_width + 2 * head_dim].reshape(d_model, 2 * head_dim), preferred_element_type=jnp.float32)
        k_rope = rope(kv[:, :head_dim]).astype(jnp.bfloat16)
        v_proj = kv[:, head_dim:].astype(jnp.bfloat16)
        k_ref[p] = k_rope
        v_ref[p] = v_proj
        length = len_ref[p]
        allowed = (col <= row) & (col < length)
        live = row < length
        for head in range(q_width // head_dim):
            at = slice(head * head_dim, (head + 1) * head_dim)
            q = jnp.dot(normed, w_v[:, 0:depth, at].reshape(d_model, head_dim), preferred_element_type=jnp.float32)
            q_rope = (rope(q) * head_dim ** -0.5).astype(jnp.bfloat16)
            scores = lax.dot_general(q_rope, k_rope, (((1,), (1,)), ((), ())), preferred_element_type=jnp.float32)
            scores = jnp.where(allowed, scores, -1e30)
            exp_scores = jnp.exp(scores - jnp.max(scores, axis=-1, keepdims=True))
            probs = exp_scores * (1.0 / jnp.sum(exp_scores, axis=-1, keepdims=True))
            probs = jnp.where(live, probs, 0.0).astype(jnp.bfloat16)
            o_v[:, at] = jnp.dot(probs, v_proj, preferred_element_type=jnp.float32).astype(jnp.bfloat16)
        w_o = w_v[:, 0:depth, q_width + 2 * head_dim:].reshape(q_width, d_model)
        mixed = h_f + jnp.dot(o_v[...], w_o, preferred_element_type=jnp.float32)
        m_v[tok, :] = mixed.astype(jnp.bfloat16)
        pltpu.make_async_copy(m_v.at[tok], m_ref.at[tok], msem.at[p]).start()
        return carry

    lax.fori_loop(0, n_seq, prompt, 0)
    comm.stage_c(1)
    for p in range(n_seq):
        tok = pl.ds(p * seq_len, seq_len)
        pltpu.make_async_copy(m_v.at[tok], m_ref.at[tok], msem.at[p]).wait()
    comm.drain(count)
    if layer == 0:
        first.drain(1)


def attn_call(layer, lengths, mlp_weights, attn_weights, full, hidden, seq_len):
    n_tok, d_model = hidden.shape
    n_seq = n_tok // seq_len
    w_gate, w_q = mlp_weights[0], attn_weights[0]
    n_layers, depth, q_width = w_q.shape
    cols = w_gate.shape[2] // CHUNKS
    rows = 2 * depth + 2 * cols // N_DEV
    piece = (depth + GAIN_ROWS, q_width + 2 * HEAD_DIM + d_model)
    cos_tab, sin_tab = rope_tables(seq_len)
    any_spec, vmem_spec = pl.BlockSpec(memory_space=pl.ANY), pl.BlockSpec(memory_space=pltpu.VMEM)
    out_shape = [jax.ShapeDtypeStruct((n_tok, d_model), jnp.bfloat16),
                 jax.ShapeDtypeStruct((n_seq, seq_len, HEAD_DIM), jnp.bfloat16),
                 jax.ShapeDtypeStruct((n_seq, seq_len, HEAD_DIM), jnp.bfloat16),
                 jax.ShapeDtypeStruct((1, d_model), jnp.float32),
                 jax.ShapeDtypeStruct((PRE, N_DEV, rows, cols), jnp.bfloat16)]
    out_specs = [any_spec, vmem_spec, vmem_spec, vmem_spec, any_spec]
    scratch = [
        pltpu.VMEM((N_DEV,) + piece, jnp.bfloat16),
        pltpu.VMEM((n_tok, d_model), jnp.bfloat16),
        pltpu.VMEM((n_tok, d_model), jnp.bfloat16),
        pltpu.VMEM((seq_len, q_width), jnp.bfloat16),
        pltpu.SemaphoreType.DMA((KINDS, PRE)),
        pltpu.SemaphoreType.DMA((KINDS, PRE)),
        pltpu.SemaphoreType.DMA,
        pltpu.SemaphoreType.DMA,
        pltpu.SemaphoreType.DMA((n_seq,)),
    ]
    if layer == 0:
        out_shape.append(jax.ShapeDtypeStruct((1, N_DEV) + piece, jnp.bfloat16))
        out_specs.append(any_spec)
        scratch += [pltpu.SemaphoreType.DMA((KINDS, 1))] * 2
        full = hidden
    return pl.pallas_call(
        functools.partial(attn_kernel, layer, n_layers),
        out_shape=out_shape,
        in_specs=[pl.BlockSpec(memory_space=pltpu.SMEM)] + [any_spec] * 10 + [vmem_spec] * 2,
        out_specs=out_specs,
        scratch_shapes=scratch,
        compiler_params=pltpu.CompilerParams(collective_id=2 + layer, has_side_effects=True, vmem_limit_bytes=63 * 1024 * 1024),
        cost_estimate=pl.CostEstimate(flops=2 * n_tok * d_model * piece[1], bytes_accessed=8 * n_tok * d_model, transcendentals=0),
        name=f'attn_gather_{layer}',
    )(lengths, *mlp_weights, *attn_weights, full, hidden, cos_tab, sin_tab)[:5]


def mlp_kernel(layer, n_own, n_layers, wg_ref, wu_ref, wd_ref, wq_ref, wk_ref, wv_ref, wo_ref, ng_ref, pre_ref, m_ref, gain_ref, out_ref, gat_ref, *rest):
    more = layer + 1 < n_layers
    if more:
        attn_gat, acc, r2, wbuf, stage, ssem, rsem, ldsem, iosem, att_s, att_r = rest
    else:
        acc, r2, wbuf, stage, ssem, rsem, ldsem, iosem = rest
    me = lax.axis_index('w')
    depth = wg_ref.shape[1]
    width = r2.shape[1]
    n_tok = r2.shape[0]
    cols = wbuf.shape[2]
    wide = cols // N_DEV
    n_steps = PRE + n_own
    mlp_refs = wg_ref, wu_ref, wd_ref
    attn_refs = wq_ref, wk_ref, wv_ref, wo_ref, ng_ref
    comm = Gather(gat_ref, ssem, rsem, gat_ref.shape[2] // 2)
    greet()
    if more:
        after = Gather(attn_gat, att_s, att_r, depth // 2)

    def stage_a(k):
        comm.stage_a(k, functools.partial(chunk_parts, layer, PRE + k, mlp_refs))

    def load_gathered(ref, at, chunk):
        chunk_parts(layer, chunk, mlp_refs, wbuf.at[me], lambda src, dst: pltpu.make_async_copy(src, dst, ldsem).start())
        for delta in range(1, N_DEV):
            pltpu.make_async_copy(ref.at[at, me ^ delta], wbuf.at[me ^ delta], ldsem).start()

    stage_a(0)
    stage_a(1)

    gain = 1.0 + gain_ref[...]

    def norm_tile(i, carry):
        tok = pl.ds(pl.multiple_of(i * TILE, TILE), TILE)
        copy = pltpu.make_async_copy(m_ref.at[tok], stage, iosem)
        copy.start()
        copy.wait()
        m_f = stage[...].astype(jnp.float32)
        acc[tok, :] = m_f
        mean_sq = jnp.mean(m_f * m_f, axis=-1, keepdims=True)
        r2[tok, :] = (m_f * lax.rsqrt(mean_sq + RMS_EPS) * gain).astype(jnp.bfloat16)
        return carry

    lax.fori_loop(0, n_tok // TILE, norm_tile, 0)

    def step(s, carry):
        k = s - PRE
        event = k + 1
        last = s == n_steps - 1
        tail = n_own - 1
        handled = n_own if more else tail

        @pl.when((event >= 0) & (event < handled))
        def _():
            comm.stage_b(event)

        if more:
            @pl.when((event >= 0) & (event + 2 < n_own))
            def _():
                stage_a(event + 2)

            @pl.when(event + 2 == n_own)
            def _():
                after.stage_a(0, functools.partial(attn_parts, layer + 1, attn_refs))

            @pl.when(event == n_own)
            def _():
                after.stage_b(0)
        else:
            @pl.when((event >= 0) & ((event + 2 < tail) | (event + 1 == tail)))
            def _():
                stage_a(jnp.where(event + 1 == tail, tail, event + 2))

        @pl.when(event >= 1)
        def _():
            comm.stage_c(event - 1)

        @pl.when(k >= 0)
        def _():
            load_gathered(gat_ref, k, s)

        @pl.when(k < 0)
        def _():
            load_gathered(pre_ref, s, s)

        pltpu.make_async_copy(gat_ref.at[0], wbuf, ldsem).wait()

        def tile_step(i, inner):
            tok = pl.ds(pl.multiple_of(i * TILE, TILE), TILE)
            if not more:
                @pl.when((event == tail) & (i == n_tok // TILE // 2))
                def _():
                    comm.stage_b(tail)

            r_t = r2[tok, :]
            gate = jnp.dot(r_t, wbuf[:, 0:depth, :].reshape(width, cols), preferred_element_type=jnp.float32)
            up = jnp.dot(r_t, wbuf[:, depth:2 * depth, :].reshape(width, cols), preferred_element_type=jnp.float32)
            act = (jax.nn.gelu(gate, approximate=True) * up).astype(jnp.bfloat16)
            for side in range(2):
                lo = 2 * depth + side * wide
                w_down = wbuf[:, lo:lo + wide, :].reshape(N_DEV * wide, cols)
                acc[tok, pl.ds(side * cols, cols)] += jnp.dot(act, w_down, preferred_element_type=jnp.float32)

            @pl.when(last)
            def _():
                @pl.when(i > 0)
                def _():
                    pltpu.make_async_copy(stage, out_ref.at[tok], iosem).wait()
                stage[...] = acc[tok, :].astype(jnp.bfloat16)
                pltpu.make_async_copy(stage, out_ref.at[tok], iosem).start()
            return inner

        lax.fori_loop(0, n_tok // TILE, tile_step, 0)
        return carry

    lax.fori_loop(0, n_steps, step, 0)
    pltpu.make_async_copy(stage, out_ref.at[pl.ds(0, TILE)], iosem).wait()

    if more:
        after.stage_c(0)
        after.drain(1)
    comm.drain(n_own)


def mlp_call(layer, mlp_weights, attn_weights, pre, mixed, gain):
    n_tok, d_model = mixed.shape
    n_layers, depth, d_ff = mlp_weights[0].shape
    cols = d_ff // CHUNKS
    rows = 2 * depth + 2 * cols // N_DEV
    n_own = CHUNKS - PRE
    any_spec = pl.BlockSpec(memory_space=pl.ANY)
    out_shape = [jax.ShapeDtypeStruct((n_tok, d_model), jnp.bfloat16),
                 jax.ShapeDtypeStruct((n_own, N_DEV, rows, cols), jnp.bfloat16)]
    scratch = [
        pltpu.VMEM((n_tok, d_model), jnp.float32),
        pltpu.VMEM((n_tok, d_model), jnp.bfloat16),
        pltpu.VMEM((N_DEV, rows, cols), jnp.bfloat16),
        pltpu.VMEM((TILE, d_model), jnp.bfloat16),
        pltpu.SemaphoreType.DMA((KINDS, n_own)),
        pltpu.SemaphoreType.DMA((KINDS, n_own)),
        pltpu.SemaphoreType.DMA,
        pltpu.SemaphoreType.DMA,
    ]
    if layer + 1 < n_layers:
        width = sum(weight.shape[2] for weight in attn_weights[:-1])
        out_shape.append(jax.ShapeDtypeStruct((1, N_DEV, depth + GAIN_ROWS, width), jnp.bfloat16))
        scratch += [pltpu.SemaphoreType.DMA((KINDS, 1))] * 2
    outs = pl.pallas_call(
        functools.partial(mlp_kernel, layer, n_own, n_layers),
        out_shape=out_shape,
        in_specs=[any_spec] * 10 + [pl.BlockSpec(memory_space=pltpu.VMEM)],
        out_specs=[any_spec] * len(out_shape),
        scratch_shapes=scratch,
        compiler_params=pltpu.CompilerParams(collective_id=layer, has_side_effects=True, vmem_limit_bytes=63 * 1024 * 1024),
        cost_estimate=pl.CostEstimate(flops=6 * n_tok * d_model * d_ff, bytes_accessed=12 * d_model * d_ff, transcendentals=0),
        name=f'mlp_gather_{layer}',
    )(*mlp_weights, *attn_weights, pre, mixed, gain)
    return outs[0], outs[-1]


def solution(mesh):
    batch_spec = P(('dp', 'w'))
    weight_spec = P(None, 'w')
    cache_spec = P(None, ('dp', 'w'))

    def device_fn(hidden, lengths, attn_norm, w_q, w_k, w_v, w_o, mlp_norm, w_gate, w_up, w_down):
        n_layers = w_q.shape[0]
        n_seq, seq_len, d_model = hidden.shape
        mlp_weights = (w_gate, w_up, w_down)
        width = sum(weight.shape[2] for weight in (w_q, w_k, w_v, w_o))
        own_gains = jnp.concatenate([attn_norm, mlp_norm], axis=0)
        own_gains = jnp.pad(own_gains, ((0, GAIN_ROWS - 2 * n_layers), (0, width - own_gains.shape[1])))
        attn_weights = (w_q, w_k, w_v, w_o, own_gains)
        k_list = []
        v_list = []
        full = None
        state = hidden.reshape(n_seq * seq_len, d_model)
        for layer in range(n_layers):
            mixed, k_rope, v_proj, gain, pre = attn_call(layer, lengths, mlp_weights, attn_weights, full, state, seq_len)
            state, full = mlp_call(layer, mlp_weights, attn_weights, pre, mixed, gain)
            k_list.append(k_rope[:, :, None, :])
            v_list.append(v_proj[:, :, None, :])
        return state.reshape(hidden.shape), jnp.stack(k_list), jnp.stack(v_list)

    return jax.shard_map(device_fn, mesh=mesh, in_specs=(batch_spec, batch_spec) + (weight_spec,) * 9, out_specs=(batch_spec, cache_spec, cache_spec), check_vma=False)
```

time: 2250 us -> 1900 us (0.84)
  Pallas kernels: 0 us -> 1880 us
  matrix products: 1150 us -> 0 us
  waiting for transfers between devices: 881 us -> 0 us
  local copies, waits for them, and re-layouts: 96.9 us -> 8.44 us
  blocking collectives: 46.7 us -> 0 us
  other arithmetic: 50 us -> 7.12 us
    pallas_call x0 -> x4, Pallas kernels: none -> 1880 us  [the longest x2 1560 us: mlp_call(): pl.pallas_call(functools.partial(mlp_kernel, layer, n_own, n_layers), out...]
    dot_general x18 -> x0, matrix products: 1150 us -> none  [the longest x2 377 us: mlp_block(): jnp.einsum('bsd,df->bsf', normed, wg_full, preferred_element_type=jnp.flo...]
    all_gather x14 -> x0, waiting for transfers between devices: 877 us -> none  [device_fn(): lax.all_gather(weight[layer_idx], 'w', axis=0, tiled=True)]
    slice x11 -> x0, local copies, waits for them, and re-layouts: 61.2 us -> none  [the longest x9 44 us: device_fn(): weight[layer_idx]]
    all_gather x4 -> x0, blocking collectives: 46.7 us -> none  [device_fn(): lax.all_gather(weight[layer_idx], 'w', axis=0, tiled=True)]
    unnamed x62 -> x1, local copies, waits for them, and re-layouts: 35.4 us -> 8.44 us
    reduce_sum x3 -> x0, other arithmetic: 24.4 us -> none  [the longest x2 19.3 us: attention(): attn_probs = exp_scores / jnp.sum(exp_scores, axis=-1, keepdims=True)]
  transfers between devices with their start and end apart: 14 -> 0, of which waited for: 6 -> 0; matrix products, arithmetic and copies ran while one was open for 51% -> 0% of each run, Pallas kernels for 0% -> 0%
where the time goes in v2:
time: 1900 us
  Pallas kernels  1880 us (99%)
    pallas_call x2, Pallas kernels, mlp_call(): pl.pallas_call(functools.partial(mlp_kernel, layer, n_own, n_layers), out...  1560 us
    pallas_call x2, Pallas kernels, attn_call(): pl.pallas_call(functools.partial(attn_kernel, layer, n_layers), out_shape...  321 us

profile of v2, /device:TPU:0, one launch (start us, length us, event | category | flops | bytes accessed | tf_op | source)
XLA Modules:
  0.0 1899.6 jit_solution(12897297067335653606)
XLA Ops:
  0.6 1.3 fusion.7.ng_ref
  2.0 1.2 fusion.3
  3.2 202.1 %attn_gather_0.1 = (bf16[2048,2048]{1,0:T(8,128)(2,1)}, bf16[8,256,256]{2,1,0:T(8,128)(2,1)}, bf16[8,256,256]{2,1,0:T(8,128)(2,1)}, f32[1,2048]{1,0:T(1,128)}, b...) custom-call(s32[8]{0:T(128)} %len_ref.3, bf16[2,256,16384]{2,1,0:T(8,128)(2,1)} %wg_ref.7, ...), custom_call_target="tpu_custom_call" | custom-call | flops 38654705664 | bytes 33554432 | tf_op jit(solution)/shard_map/attn_gather_0/pallas_call | solution.py:243
  205.3 807.6 %mlp_gather_0.1 = (bf16[2048,2048]{1,0:T(8,128)(2,1)}, bf16[14,8,768,1024]{3,2,1,0:T(8,128)(2,1)}, bf16[1,8,264,4608]{3,2,1,0:T(8,128)(2,1)}) custom-call(bf16[2,256,16384]{2,1,0:T(8,128)(2,1)} %wg_ref.7, bf16[2,256,16384]{2,1,0:T(8,128)(2,1)} %wu_ref.7, bf16[2,2048,2048]{2,1,0:T(8,128)(2,1)} %wd_ref.7, bf16[2,256,2048]{2,1,0:T(8,128)(2,1)} %wq_ref.7, ...), custom_call_target="tpu_custom_call" | custom-call | flops 412316860416 | bytes 402653184 | tf_op jit(solution)/shard_map/mlp_gather_0/pallas_call | solution.py:403
  1013.0 118.8 %attn_gather_1.1 = (bf16[2048,2048]{1,0:T(8,128)(2,1)}, bf16[8,256,256]{2,1,0:T(8,128)(2,1)}, bf16[8,256,256]{2,1,0:T(8,128)(2,1)}, f32[1,2048]{1,0:T(1,128)}, bf16[2,8,768,1024]{3,2,1,0:T(8,128)(2,1)}) custom-call(s32[8]{0:T(128)} %len_ref.3, bf16[2,256,16384]{2,1,0:T(8,128)(2,1)} %wg_ref.7, bf16[2,256,16384]{2,1,0:T(8,128)(2,1)} %wu_ref.7, ...), custom_call_target="tpu_custom_call" | custom-call | flops 38654705664 | bytes 33554432 | tf_op jit(solution)/shard_map/attn_gather_1/pallas_call | solution.py:243
  1131.8 4.6 maximum_bitcast_fusion
  1136.4 754.8 %mlp_gather_1.1 = (bf16[2048,2048]{1,0:T(8,128)(2,1)}, bf16[14,8,768,1024]{3,2,1,0:T(8,128)(2,1)}) custom-call(bf16[2,256,16384]{2,1,0:T(8,128)(2,1)} %wg_ref.7, bf16[2,256,16384]{2,1,0:T(8,128)(2,1)} %wu_ref.7, bf16[2,2048,2048]{2,1,0:T(8,128)(2,1)} %wd_ref.7, bf16[2,256,2048]{2,1,0:T(8,128)(2,1)} %wq_ref.7, bf16[2,256,256]{2,1,0:T(8,128)(2,1)} %wk_ref.7, ...), custom_call_target="tpu_custom_call" | custom-call | flops 412316860416 | bytes 402653184 | tf_op jit(solution)/shard_map/mlp_gather_1/pallas_call | solution.py:403
  1891.1 8.4 copy.17
  (1 shorter events, 0.0 us)
